TPU v7x, 32 devices: a whole 2x2x4 slice. The times are simulated.
32 devices in a mesh: dp: 8 (over z, y), tensor: 4 (over x, core).
Axes of the slice: x: 2, y: 2, z: 4, core: 2. Of those that a mesh axis runs over, the one named last changes fastest.
Arguments:
- hidden: bfloat16 [4096, 5120], P('dp'), may hold values from -48 to 48
- head_weight: bfloat16 [5120, 4096], P(None, 'tensor'), may hold values from -0.069877124 to 0.069877124
- token_ids: int32 [4096], P('dp'), may hold values from 0 to 4095
- old_logprob: float32 [4096], P('dp'), may hold values from -12.5 to 0.3
- rewards: int32 [64], P('dp'), may hold values from 0 to 1, as said below
- lengths: int32 [64], P('dp'), may hold values from 1 to 64, as said below
- group_ids: int32 [64], P('dp'), may hold values from 0 to 3, as said below
- loss_scale: float32 [], replicated, may hold values from 4096 to 16384
Outputs:
- loss: float32 [], replicated
- grad_hidden: float32 [4096, 5120], P('dp', 'tensor')
- grad_weight: float32 [5120, 4096], P('dp', 'tensor')
Inputs may be any that keep to these rules, and one draw needn't show every extreme that they name: `group_ids`: each group number names exactly 16 rollouts. `rewards`: some group holds both a 0 and a 1. `lengths`: some index of dp holds only rollouts of length 64 whose prompts hold both a 0 and a 1.
All inputs are finite; a program needn't handle non-finite values.
Results may differ from a plain program's by a relative error of at most 0.003.
Values may be sent and summed in bfloat16 or wider, within the bound.
A program may use at most 192 MiB of HBM per device.

v0:
```python
import jax
import jax.numpy as jnp
from jax import lax
from jax.sharding import PartitionSpec as P

GROUP = 16


clip_low = 0.2
clip_high = 0.28


def contract_rows(first_operand, second_operand):
    return lax.dot_general(
        first_operand, second_operand, (((0,), (0,)), ((), ())), preferred_element_type=jnp.float32
    )


def contract_cols(first_operand, second_operand):
    return lax.dot_general(
        first_operand, second_operand, (((1,), (1,)), ((), ())), preferred_element_type=jnp.float32
    )


def run_blocks(block_fn, initial):
    return block_fn(0, initial)


def group_terms(member, group_wins, reward_float):
    group_alive = jnp.logical_and(group_wins > 0.5, group_wins < GROUP - 0.5).astype(jnp.float32)
    center = group_wins / GROUP
    spread = jnp.where(group_alive > 0.5, jnp.sqrt(group_wins * (GROUP - group_wins)) / GROUP, 1.0)
    roll_alive = jnp.sum(member * group_alive[None, :], axis=1)
    roll_center = jnp.sum(member * center[None, :], axis=1)
    roll_spread = jnp.sum(member * spread[None, :], axis=1)
    advantage = roll_alive * (reward_float - roll_center) / roll_spread
    return (group_alive, roll_alive, advantage)


def policy_terms(log_prob, old_rows, adv_rows, weight_rows, factor):
    prob_ratio = jnp.exp(log_prob - old_rows)
    clipped = jnp.clip(prob_ratio, 1.0 - clip_low, 1.0 + clip_high)
    token_loss = -jnp.minimum(prob_ratio * adv_rows, clipped * adv_rows)
    active = prob_ratio * adv_rows <= clipped * adv_rows
    coefficient = jnp.where(active, -adv_rows * prob_ratio, 0.0) * weight_rows * factor
    return (token_loss, coefficient)


def shards(hidden, head_weight, token_ids, old_logprob, rewards, lengths, group_ids, loss_scale):
    row_count, model_width = hidden.shape
    roll_count = rewards.shape[0]
    response = row_count // roll_count
    vocab_part = head_weight.shape[1]
    data_size = lax.axis_size("dp")
    group_count = roll_count * data_size // GROUP
    member = (group_ids[:, None] == jnp.arange(group_count, dtype=jnp.int32)[None, :]).astype(
        jnp.float32
    )
    reward_float = rewards.astype(jnp.float32)
    length_float = lengths.astype(jnp.float32)
    local_wins = jnp.sum(member * reward_float[:, None], axis=0)
    group_wins = lax.psum(local_wins, "dp")
    group_alive, roll_alive, advantage = group_terms(member, group_wins, reward_float)
    token_count = lax.psum(jnp.sum(roll_alive * length_float), "dp")
    divisor = jnp.maximum(token_count, 1.0)
    factor = loss_scale / divisor
    position = jnp.arange(response, dtype=jnp.int32)
    inside = (position[None, :] < lengths[:, None]).astype(jnp.float32)
    token_weight = (roll_alive[:, None] * inside).reshape(row_count)
    token_adv = jnp.broadcast_to(advantage[:, None], (roll_count, response)).reshape(row_count)

    def logit_block(block_index, current):
        block_logits = jnp.dot(hidden, head_weight, preferred_element_type=jnp.float32)
        return block_logits

    logits = run_blocks(logit_block, jnp.zeros((row_count, vocab_part), jnp.float32))
    row_top = lax.pmax(jnp.max(logits, axis=1), "tensor")
    shifted = jnp.exp(logits - row_top[:, None])
    column = (
        jnp.arange(vocab_part, dtype=jnp.int32)[None, :] + lax.axis_index("tensor") * vocab_part
    )
    is_target = column == token_ids[:, None]
    row_total, target = lax.psum(
        (jnp.sum(shifted, axis=1), jnp.sum(jnp.where(is_target, logits, 0.0), axis=1)), "tensor"
    )
    softmax_rows = shifted / row_total[:, None]
    log_prob = target - row_top - jnp.log(row_total)
    token_loss, coefficient = policy_terms(log_prob, old_logprob, token_adv, token_weight, factor)
    logit_grad = (coefficient[:, None] * (is_target.astype(jnp.float32) - softmax_rows)).astype(
        jnp.bfloat16
    )

    def grad_block(block_index, current):
        return contract_cols(logit_grad, head_weight)

    grad_part = run_blocks(grad_block, jnp.zeros((row_count, model_width), jnp.float32))
    columns = lax.all_to_all(hidden, "dp", split_axis=1, concat_axis=0, tiled=True)
    grad_weight = contract_rows(columns, lax.all_gather(logit_grad, "dp", axis=0, tiled=True))
    grad_cols = lax.psum_scatter(grad_part, "tensor", scatter_dimension=1, tiled=True)
    loss_total = lax.psum(jnp.sum(token_weight * token_loss), "dp")
    return (loss_total / divisor, grad_cols, grad_weight)


def solution(mesh):
    return jax.shard_map(
        shards,
        mesh=mesh,
        in_specs=(
            P("dp", None),
            P(None, "tensor"),
            P("dp"),
            P("dp"),
            P("dp"),
            P("dp"),
            P("dp"),
            P(),
        ),
        out_specs=(P(), P("dp", "tensor"), P("dp", "tensor")),
        check_vma=False,
    )
```

profile of v0, /device:TPU:0, one launch (start us, length us, event | category | flops | bytes accessed | tf_op | source)
XLA Modules:
  0.0 328.7 jit_solution(15351003358301694592)
XLA Ops:
  8.0 0.0 all-gather.2.cloned.1.call-start
  8.0 0.7 convert_element_type.17
  8.7 0.8 select_reduce_fusion.3
  9.5 23.2 %psum.35 = f32[4]{0:T(128)S(1)} all-reduce(f32[4]{0:T(128)S(1)} %select_reduce_fusion.3), channel_id=1, replica_groups=mesh['dp'=8,'tensor'=4] {'dp'}, use_global_device_ids=true, to_apply=%region_1.0 | all-reduce | flops 4 | bytes 32 | tf_op jit(solution)/shard_map/psum | solution.py:62
  33.3 0.7 select_reduce_fusion.1
  34.1 0.7 fusion.5
  34.8 1.3 multiply_reduce_fusion.1
  36.1 0.1 broadcast_in_dim.12
  36.1 0.1 reshape.36
  36.2 0.1 mul.91
  36.3 0.0 copy-start.1
  36.3 10.0 %fusion.8 = (f32[512]{0:T(512)S(1)}, f32[512,1024]{1,0:T(8,128)S(1)}) fusion(bf16[512,5120]{1,0:T(8,128)(2,1)} %param.8, bf16[5120,1024]{1,0:T(8,128)(2,1)} %param.9), kind=kOutput, calls=%fused_computation.29 | convolution fusion | flops 5369232896 | bytes 17827840 | tf_op jit(solution)/shard_map/dot_general | solution.py:73
  46.3 5.7 %pmax.7 = f32[512]{0:T(512)S(1)} all-reduce(f32[512]{0:T(512)S(1)} %get-tuple-element.30), channel_id=1, replica_groups=mesh['dp'=8,'tensor'=4] {'tensor'}, use_global_device_ids=true, to_apply=%region_6.7 | all-reduce | flops 512 | bytes 4096 | tf_op jit(solution)/shard_map/pmax | solution.py:77
  52.0 0.0 copy-done
  52.0 0.7 fusion
  52.7 6.6 %all-reduce.1 = (f32[512]{0:T(512)S(1)}, f32[512]{0:T(512)S(1)}) all-reduce(f32[512]{0:T(512)S(1)} %get-tuple-element.16, f32[512]{0:T(512)S(1)} %get-tuple-element.15), channel_id=1, replica_groups=mesh['dp'=8,'tensor'=4] {'tensor'}, use_global_device_ids=true, to_apply=%region_8.9 | all-reduce | flops 1024 | bytes 8192 | tf_op jit(solution)/shard_map/psum | solution.py:83
  59.3 0.0 copy-done.1
  59.3 0.6 multiply_reduce_fusion
  59.9 17.8 %all-reduce = (f32[]{:T(128)}, f32[]{:T(128)}) all-reduce(f32[]{:T(128)} %get-tuple-element.24, f32[]{:T(128)} %get-tuple-element.26), channel_id=1, replica_groups=mesh['dp'=8,'tensor'=4] {'dp'}, use_global_device_ids=true, to_apply=%region_12.13 | all-reduce | flops 2 | bytes 16 | tf_op jit(solution)/shard_map/psum | solution.py:100
  78.4 1.6 fusion.3
  80.1 0.0 all-gather.2.cloned.1.call-update
  80.1 0.0 reduce-scatter.2.cloned.1.call-start
  80.1 10.9 %fusion.9 = f32[512,5120]{1,0:T(8,128)} fusion(bf16[512,1024]{1,0:T(8,128)(2,1)} %fusion.3, bf16[5120,1024]{1,0:T(8,128)(2,1)} %param.9), kind=kOutput, calls=%fused_computation.30 | convolution fusion | flops 5368709120 | bytes 22020096 | tf_op jit(solution)/shard_map/dot_general | solution.py:20
  91.1 0.0 reduce-scatter.2.cloned.1.call-update
  91.1 8.1 %copy.16 = bf16[512,5120]{0,1:T(8,128)(2,1)} copy(bf16[512,5120]{1,0:T(8,128)(2,1)} %param.8) | data formatting | bytes 10485760 | tf_op args[0]
  99.2 4.8 %all-to-all-start = ((bf16[512,8,640]{0,2,1:T(8,128)(2,1)}), bf16[512,8,640]{0,2,1:T(8,128)(2,1)}, u32[]{:S(2)}, u32[]{:S(2)}) async-start(bf16[512,8,640]{0,2,1:T(8,128)(2,1)} %bitcast.11), calls=%async_computation.1 | async-start | bytes 10485760 | tf_op jit(solution)/shard_map/all_to_all | solution.py:97
  104.7 194.7 %all-to-all-done = bf16[512,8,640]{0,2,1:T(8,128)(2,1)} async-done(((bf16[512,8,640]{0,2,1:T(8,128)(2,1)}), bf16[512,8,640]{0,2,1:T(8,128)(2,1)}, u32[]{:S(2)}, u32[]{:S(2)}) %all-to-all-start) | async-done | bytes 5242912 | tf_op jit(solution)/shard_map/all_to_all | solution.py:97
  299.4 7.9 %copy.17 = bf16[8,512,640]{2,1,0:T(8,128)(2,1)} copy(bf16[8,512,640]{1,2,0:T(8,128)(2,1)} %bitcast.1) | data formatting | bytes 10485760 | tf_op jit(solution)/shard_map/all_to_all | solution.py:97
  307.3 0.0 all-gather.2.cloned.1.call-done
  307.3 10.7 %convolution_bitcast_fusion = f32[640,1024]{0,1:T(8,128)S(1)} fusion(bf16[4096,1024]{1,0:T(8,128)(2,1)} %all-gather.2.cloned.1.call-done, bf16[4096,640]{1,0:T(8,128)(2,1)} %bitcast.12), kind=kOutput, calls=%fused_computation.8 | convolution fusion | flops 5368709120 | bytes 16252928 | tf_op jit(solution)/shard_map/dot_general | solution.py:14
  318.0 2.1 copy.18
  320.1 0.0 reduce-scatter.2.cloned.1.call-done
  (5 shorter events, 0.0 us)
Async XLA Ops:
  8.0 299.3 %all-gather.2.cloned.1.call-start = ((), (), s32[]{:S(2)}) async-start(), calls=%async_computation.3 | async-start | bytes 9437184 | tf_op jit(solution)/shard_map/all_gather | solution.py:98
  36.3 15.7 %copy-start = (s32[512]{0:T(512)S(1)}, s32[512]{0:T(512)}, u32[]{:S(2)}) copy-start(s32[512]{0:T(512)} %param.10) | copy-start | bytes 6148
  36.3 23.0 %copy-start.1 = (f32[512]{0:T(512)S(1)}, f32[512]{0:T(512)}, u32[]{:S(2)}) copy-start(f32[512]{0:T(512)} %param.11) | copy-start | bytes 6148
  80.1 240.0 %reduce-scatter.2.cloned.1.call-start = ((), (), s32[]{:S(2)}) async-start(), calls=%async_computation.2 | async-start | bytes 13107200 | tf_op jit(solution)/shard_map/reduce_scatter | solution.py:99
  99.2 200.2 %all-to-all-start = ((bf16[512,8,640]{0,2,1:T(8,128)(2,1)}), bf16[512,8,640]{0,2,1:T(8,128)(2,1)}, u32[]{:S(2)}, u32[]{:S(2)}) async-start(bf16[512,8,640]{0,2,1:T(8,128)(2,1)} %bitcast.11), calls=%async_computation.1 | async-start | bytes 10485760 | tf_op jit(solution)/shard_map/all_to_all | solution.py:97
Sparse Core Ops, SparseCore 0:
  80.2 224.8 all-gather.1
Sparse Core Ops, SparseCore 1:
  91.2 82.2 reduce-scatter.1
where the time goes:
time: 333 us; the launch traced here: 329 us
  waiting for transfers between devices  195 us (59%)
  blocking collectives  53.2 us (16%)
  matrix products  31.7 us (10%)
  between operations  18.7 us (6%)
  local copies, waits for them, and re-layouts  18.3 us (5%)
  other arithmetic  7.13 us (2%)
  starting transfers between devices  4.9 us (1%)
    all_to_all x1, waiting for transfers between devices, shards(): lax.all_to_all(hidden, 'dp', split_axis=1, concat_axis=0, tiled=True)  195 us
    psum x1, blocking collectives, shards(): group_wins = lax.psum(local_wins, 'dp')  23.2 us
    psum x1, blocking collectives, shards(): loss_total = lax.psum(jnp.sum(token_weight * token_loss), 'dp')  17.8 us
    dot_general x1, matrix products, contract_cols(): lax.dot_general(first_operand, second_operand, (((1,), (1,)), ((), ())),...  10.9 us
    dot_general x1, matrix products, contract_rows(): lax.dot_general(first_operand, second_operand, (((0,), (0,)), ((), ())),...  10.7 us
    unnamed x6, local copies, waits for them, and re-layouts  10.2 us
    dot_general x1, matrix products, logit_block(): jnp.dot(hidden, head_weight, preferred_element_type=jnp.float32)  10 us
    all_to_all x1, local copies, waits for them, and re-layouts, shards(): lax.all_to_all(hidden, 'dp', split_axis=1, concat_axis=0, tiled=True)  7.87 us
  transfers between devices with their start and end apart: 3, of which 1 were waited for; matrix products, arithmetic and copies ran while one was open for 12% of the time, Pallas kernels for 0%

commit v1 on v0

v1 whole, which is shorter than its diff:
```python
import functools

import jax
import jax.numpy as jnp
from jax import lax
from jax.experimental import pallas as pl
from jax.experimental.pallas import tpu as pltpu
from jax.sharding import PartitionSpec as P

GROUP = 16
clip_low = 0.2
clip_high = 0.28
MESH = pl.DeviceIdType.MESH
F32 = jnp.float32
BF16 = jnp.bfloat16


def kernel(cfg, hidden, hsrc, w, rows, info, loss_o, gh_o, gw_o,
           hid_v, w_v, logits, cols, stats, info_all, loss_all, lg_all, hcol, rs_recv,
           ld, s_info, r_info, s_hid, r_hid, s_x, r_x, s_d, r_d, s_st, r_st,
           s_loss, r_loss, s_rs, r_rs, s_a, s_b, r_lg):
    dp, T, nA, nB, sliced = cfg
    R, D = hid_v.shape
    V = w_v.shape[1]
    Q = R // T
    C = D // dp
    CT = D // T
    nX = T // 2
    NK = 8
    KC = D // NK
    me = lax.axis_index("dp")
    t = lax.axis_index("tensor")
    a, b = me // nB, me % nB
    x, c = t // 2, t % 2

    def rcopy(src, dst, ss, rs, dev):
        return pltpu.make_async_remote_copy(
            src_ref=src, dst_ref=dst, send_sem=ss, recv_sem=rs, device_id=dev, device_id_type=MESH
        )

    def load_h(k):
        s = pl.ds(pl.multiple_of(k * KC, KC), KC)
        return pltpu.make_async_copy(hidden.at[:, s], hid_v.at[:, s], ld.at[0, k])

    def load_w(k):
        s = pl.ds(pl.multiple_of(k * KC, KC), KC)
        return pltpu.make_async_copy(w.at[s], w_v.at[s], ld.at[1, k])

    for k in range(NK):
        load_h(k).start()
        load_w(k).start()

    barrier = pltpu.get_barrier_semaphore()
    for d in range(1, dp):
        pl.semaphore_signal(barrier, inc=1, device_id={"dp": (me + d) % dp}, device_id_type=MESH)
    for d in range(1, T):
        pl.semaphore_signal(barrier, inc=1, device_id={"tensor": (t + d) % T}, device_id_type=MESH)
    pl.semaphore_wait(barrier, dp - 1 + T - 1)

    def qrows(q):
        return pl.ds(pl.multiple_of(q * Q, Q), Q)

    def hslice(j):
        if sliced:
            return hsrc.at[qrows(t), pl.ds(pl.multiple_of(j * C, C), C)]
        return hsrc.at[j, qrows(t), :]

    def c_info(d):
        j = (me + d) % dp
        return rcopy(info, info_all.at[me], s_info.at[d], r_info.at[me], {"dp": j})

    def c_hid(d):
        j = (me + d) % dp
        return rcopy(hslice(j), hcol.at[me, qrows(t), :], s_hid.at[d], r_hid.at[me], {"dp": j})

    for d in range(1, dp):
        c_info(d).start()
    for d in range(1, dp):
        c_hid(d).start()
    own_hid = pltpu.make_async_copy(hslice(me), hcol.at[me, qrows(t), :], s_hid.at[0])
    own_hid.start()
    info_all[me] = info[...]

    pad = jnp.zeros((128 - rows.shape[0], R), F32)
    cols[...] = jnp.transpose(jnp.concatenate([rows[...], pad], axis=0))

    logits[...] = jnp.zeros_like(logits)

    @pl.loop(0, NK)
    def _(k):
        s = pl.ds(pl.multiple_of(k * KC, KC), KC)
        load_h(k).wait()
        load_w(k).wait()
        logits[...] += jnp.dot(hid_v[:, s], w_v[s, :], preferred_element_type=F32)

    RC = 32
    lane = lax.broadcasted_iota(jnp.int32, (RC, 128), 1)
    vcol = lax.broadcasted_iota(jnp.int32, (RC, V), 1).astype(F32) + (t * V).astype(F32)

    @pl.loop(0, R // RC)
    def _(n):
        r = pl.ds(pl.multiple_of(n * RC, RC), RC)
        lo = logits[r, :]
        tok = cols[r, 0:1]
        top = jnp.max(lo, axis=1, keepdims=True)
        target = jnp.sum(jnp.where(vcol == tok, lo, 0.0), axis=1, keepdims=True)
        e = jnp.exp(lo - top)
        total = jnp.sum(e, axis=1, keepdims=True)
        logits[r, :] = e
        cols[r, :] = jnp.where(
            lane == 0, tok, jnp.where(lane == 1, top, jnp.where(lane == 2, total, jnp.where(lane == 3, target, 0.0)))
        )

    stats[t] = jnp.transpose(cols[...])[0:8, :]

    def c_st(d):
        return rcopy(stats.at[t], stats.at[t], s_st.at[d], r_st.at[t], {"tensor": (t + d) % T})

    for d in range(1, T):
        c_st(d).start()
    for d in range(1, dp):
        i = (me + d) % dp
        rcopy(info, info_all.at[i], s_info.at[d], r_info.at[i], {"dp": i}).wait_recv()
    wins2 = info_all[0]
    for i in range(1, dp):
        wins2 = wins2 + info_all[i]
    G8 = info.shape[0] - 8
    wins = wins2[0:G8, 0:1]
    lens = wins2[0:G8, 1:2]
    alive = jnp.logical_and(wins > 0.5, wins < GROUP - 0.5).astype(F32)
    center = wins / GROUP
    spread = jnp.where(alive > 0.5, jnp.sqrt(wins * (GROUP - wins)) / GROUP, 1.0)
    token_count = jnp.sum(alive * lens, axis=0, keepdims=True)
    divisor = jnp.maximum(token_count, 1.0)
    factor = info[G8 : G8 + 1, 0:1] / divisor
    old = rows[1:2, :]
    gid = rows[2:3, :]
    rew = rows[3:4, :]
    inside = rows[4:5, :]
    member = (lax.broadcasted_iota(jnp.int32, (G8, R), 0).astype(F32) == gid).astype(F32)
    roll_alive = jnp.sum(member * alive, axis=0, keepdims=True)
    roll_center = jnp.sum(member * center, axis=0, keepdims=True)
    roll_spread = jnp.sum(member * spread, axis=0, keepdims=True)
    adv = roll_alive * (rew - roll_center) / roll_spread
    weight = roll_alive * inside

    for d in range(1, T):
        i = (t + d) % T
        rcopy(stats.at[i], stats.at[i], s_st.at[d], r_st.at[i], {"tensor": i}).wait_recv()
    top = stats[0, 1:2, :]
    for i in range(1, T):
        top = jnp.maximum(top, stats[i, 1:2, :])
    total = jnp.zeros_like(top)
    target = jnp.zeros_like(top)
    for i in range(T):
        total = total + stats[i, 2:3, :] * jnp.exp(stats[i, 1:2, :] - top)
        target = target + stats[i, 3:4, :]
    log_prob = target - top - jnp.log(total)
    ratio = jnp.exp(log_prob - old)
    clipped = jnp.clip(ratio, 1.0 - clip_low, 1.0 + clip_high)
    token_loss = -jnp.minimum(ratio * adv, clipped * adv)
    active = ratio * adv <= clipped * adv
    coef = jnp.where(active, -adv * ratio, 0.0) * weight * factor
    mytop = stats[t][1:2, :]
    scale = jnp.exp(mytop - top) / total
    loss_all[me] = jnp.broadcast_to(jnp.sum(weight * token_loss, axis=1, keepdims=True), (8, 128))
    cols[...] = jnp.transpose(
        jnp.concatenate([rows[0:1, :], coef, scale, jnp.zeros((125, R), F32)], axis=0)
    )

    @pl.loop(0, R // RC)
    def _(n):
        r = pl.ds(pl.multiple_of(n * RC, RC), RC)
        hit = jnp.where(vcol == cols[r, 0:1], 1.0, 0.0)
        lg_all[me, r, :] = (cols[r, 1:2] * (hit - logits[r, :] * cols[r, 2:3])).astype(BF16)

    def c_up(j):
        return rcopy(lg_all.at[j], lg_all.at[j], s_a.at[0, j], r_lg.at[j], {"dp": me + nB})

    def c_down(j):
        return rcopy(lg_all.at[j], lg_all.at[j], s_a.at[1, j], r_lg.at[j], {"dp": me - nB})

    def c_b(j, d):
        return rcopy(lg_all.at[j], lg_all.at[j], s_b.at[d, j], r_lg.at[j], {"dp": a * nB + (b + d) % nB})

    def recv_lg(j):
        rcopy(lg_all.at[j], lg_all.at[j], s_a.at[0, j], r_lg.at[j], {"dp": (me + 1) % dp}).wait_recv()

    def send_b(j):
        for d in range(1, nB):
            c_b(j, d).start()

    @pl.when(a < nA - 1)
    def _():
        c_up(me).start()

    @pl.when(a > 0)
    def _():
        c_down(me).start()

    send_b(me)

    def c_loss(d):
        return rcopy(loss_all.at[me], loss_all.at[me], s_loss.at[d], r_loss.at[me], {"dp": (me + d) % dp})

    for d in range(1, dp):
        c_loss(d).start()

    GC = 640 if CT % 640 == 0 else CT
    per = CT // GC

    def gh_dot(col0):
        return lax.dot_general(
            lg_all[me], w_v[pl.ds(col0, GC), :], (((1,), (1,)), ((), ())), preferred_element_type=F32
        )

    @pl.loop(0, (T - 1) * per)
    def _(n):
        peer = (t + 1 + n // per) % T
        col0 = pl.multiple_of(peer * CT + (n % per) * GC, GC)
        hid_v[:, pl.ds(col0, GC)] = gh_dot(col0).astype(BF16)

    own_hid.wait()
    for d in range(1, dp):
        i = (me + d) % dp
        rcopy(hslice(i), hcol.at[i, qrows(t), :], s_hid.at[d], r_hid.at[i], {"dp": i}).wait_recv()

    def c_x(d):
        q = hcol.at[:, qrows(t), :]
        return rcopy(q, q, s_x.at[d], r_x.at[x], {"tensor": ((x + d) % nX) * 2 + c})

    def c_d(xx):
        q = hcol.at[:, qrows(2 * xx + c), :]
        return rcopy(q, q, s_d.at[xx], r_d.at[xx], {"tensor": 2 * x + 1 - c})

    for d in range(1, nX):
        c_x(d).start()
    c_d(x).start()

    def c_rs(d):
        peer = (t + d) % T
        return rcopy(
            hid_v.at[:, pl.ds(pl.multiple_of(peer * CT, CT), CT)],
            rs_recv.at[t], s_rs.at[d], r_rs.at[t], {"tensor": peer},
        )

    for d in range(1, T):
        c_rs(d).start()

    @pl.loop(0, per)
    def _(n):
        off = pl.multiple_of(n * GC, GC)
        gh_o[:, pl.ds(off, GC)] = gh_dot(pl.multiple_of(t * CT + off, GC))

    def relay(s):
        @pl.when(a >= s)
        def _():
            j = me - s * nB
            recv_lg(j)

            @pl.when(a < nA - 1)
            def _():
                c_up(j).start()

            send_b(j)

        @pl.when(a + s < nA)
        def _():
            j = me + s * nB
            recv_lg(j)

            @pl.when(a > 0)
            def _():
                c_down(j).start()

            send_b(j)

    def gw_add(j):
        gw_o[...] += lax.dot_general(
            hcol[j], lg_all[j], (((0,), (0,)), ((), ())), preferred_element_type=F32
        )

    gw_o[...] = jnp.zeros_like(gw_o)

    def add_steps(items):
        for s, d in items:
            @pl.loop(0, 1 if s == 0 else 2)
            def _(k):
                aa = a + (2 * k - 1) * s
                j = aa * nB + (b + d) % nB

                @pl.when(jnp.logical_and(aa >= 0, aa < nA))
                def _():
                    if d > 0:
                        recv_lg(j)
                    gw_add(j)

    relay(1)
    relay(2)
    for d in range(1, nX):
        xx = (x + d) % nX
        q = hcol.at[:, qrows(2 * xx + c), :]
        rcopy(q, q, s_x.at[d], r_x.at[xx], {"tensor": 2 * xx + c}).wait_recv()
        c_d(xx).start()
    for xx in range(nX):
        q = hcol.at[:, qrows(2 * xx + 1 - c), :]
        rcopy(q, q, s_d.at[xx], r_d.at[xx], {"tensor": 2 * x + 1 - c}).wait_recv()
    add_steps([(0, 0), (1, 0), (2, 0)] + [(0, d) for d in range(1, nB)])
    for s in range(3, nA):
        relay(s)
        add_steps([(s, 0)])
    for s in range(1, nA - 1):
        add_steps([(s, d) for d in range(1, nB)])

    for d in range(1, T):
        i = (t + d) % T
        rcopy(hid_v.at[:, pl.ds(0, CT)], rs_recv.at[i], s_rs.at[d], r_rs.at[i], {"tensor": i}).wait_recv()

    @pl.loop(0, R // RC)
    def _(n):
        r = pl.ds(pl.multiple_of(n * RC, RC), RC)
        acc = gh_o[r, :]
        for d in range(1, T):
            acc = acc + rs_recv[(t + d) % T, r, :].astype(F32)
        gh_o[r, :] = acc

    for d in range(1, dp):
        i = (me + d) % dp
        rcopy(loss_all.at[i], loss_all.at[i], s_loss.at[d], r_loss.at[i], {"dp": i}).wait_recv()
    loss = loss_all[0]
    for i in range(1, dp):
        loss = loss + loss_all[i]
    loss_o[...] = loss / divisor

    add_steps([(nA - 1, d) for d in range(1, nB)])

    for d in range(1, dp):
        c_info(d).wait_send()
        c_hid(d).wait_send()
        c_loss(d).wait_send()
    for d in range(1, T):
        c_st(d).wait_send()
        c_rs(d).wait_send()
    for d in range(1, nX):
        c_x(d).wait_send()
    for xx in range(nX):
        c_d(xx).wait_send()
    for s in range(nA):
        @pl.when(a >= s)
        def _():
            j = me - s * nB

            @pl.when(a < nA - 1)
            def _():
                c_up(j).wait_send()

            for d in range(1, nB):
                c_b(j, d).wait_send()

        @pl.when(a + s < nA)
        def _():
            j = me + s * nB

            @pl.when(a > 0)
            def _():
                c_down(j).wait_send()

            if s > 0:
                for d in range(1, nB):
                    c_b(j, d).wait_send()


def shards(hidden, head_weight, token_ids, old_logprob, rewards, lengths, group_ids, loss_scale):
    R, D = hidden.shape
    V = head_weight.shape[1]
    rolls = rewards.shape[0]
    dp = lax.axis_size("dp")
    T = lax.axis_size("tensor")
    nA = 4 if dp % 4 == 0 else dp
    nB = dp // nA
    groups = rolls * dp // GROUP
    G8 = -(-groups // 8) * 8
    C = D // dp
    sliced = C % 128 == 0
    response = R // rolls
    member = (group_ids[None, :] == jnp.arange(G8, dtype=jnp.int32)[:, None]).astype(F32)
    wins = jnp.sum(member * rewards.astype(F32)[None, :], axis=1)
    lens = jnp.sum(member * lengths.astype(F32)[None, :], axis=1)
    lane = jnp.arange(128)[None, :]
    info = jnp.where(lane == 0, wins[:, None], jnp.where(lane == 1, lens[:, None], 0.0))
    info = jnp.concatenate([info, jnp.full((8, 128), 1.0, F32) * loss_scale], axis=0)
    inside = (jnp.arange(response, dtype=jnp.int32)[None, :] < lengths[:, None]).astype(F32).reshape(R)
    spread = lambda v: jnp.broadcast_to(v.astype(F32)[:, None], (rolls, response)).reshape(R)
    zero = jnp.zeros((R,), F32)
    rows = jnp.stack(
        [token_ids.astype(F32), old_logprob, spread(group_ids), spread(rewards), inside, zero, zero, zero]
    )
    if sliced:
        hsrc = hidden
    else:
        hsrc = jnp.transpose(hidden.reshape(R, dp, C), (1, 0, 2))
    vm = pl.BlockSpec(memory_space=pltpu.VMEM)
    anyw = pl.BlockSpec(memory_space=pl.ANY)
    dma = pltpu.SemaphoreType.DMA
    loss, gh, gw = pl.pallas_call(
        functools.partial(kernel, (dp, T, nA, nB, sliced)),
        out_shape=(
            jax.ShapeDtypeStruct((8, 128), F32),
            jax.ShapeDtypeStruct((R, D // T), F32),
            jax.ShapeDtypeStruct((C, V), F32),
        ),
        in_specs=[anyw, anyw, anyw, vm, vm],
        out_specs=(vm, vm, vm),
        scratch_shapes=[
            pltpu.VMEM((R, D), BF16),
            pltpu.VMEM((D, V), BF16),
            pltpu.VMEM((R, V), F32),
            pltpu.VMEM((R, 128), F32),
            pltpu.VMEM((T, 8, R), F32),
            pltpu.VMEM((dp, G8 + 8, 128), F32),
            pltpu.VMEM((dp, 8, 128), F32),
            pltpu.VMEM((dp, R, V), BF16),
            pltpu.VMEM((dp, R, C), BF16),
            pltpu.VMEM((T, R, D // T), BF16),
            dma((2, 8)),
            dma((dp,)), dma((dp,)),
            dma((dp,)), dma((dp,)),
            dma((T,)), dma((T,)),
            dma((T,)), dma((T,)),
            dma((T,)), dma((T,)),
            dma((dp,)), dma((dp,)),
            dma((T,)), dma((T,)),
            dma((2, dp)), dma((nB, dp)), dma((dp,)),
        ],
        compiler_params=pltpu.CompilerParams(
            collective_id=0, has_side_effects=True, vmem_limit_bytes=63 * 1024 * 1024
        ),
    )(hidden, hsrc, head_weight, rows, info)
    return (loss[0, 0], gh, gw)


def solution(mesh):
    return jax.shard_map(
        shards,
        mesh=mesh,
        in_specs=(
            P("dp", None),
            P(None, "tensor"),
            P("dp"),
            P("dp"),
            P("dp"),
            P("dp"),
            P("dp"),
            P(),
        ),
        out_specs=(P(), P("dp", "tensor"), P("dp", "tensor")),
        check_vma=False,
    )
```

time: 333 us -> 148 us (0.44); the launches traced: 329 us -> 148 us
  waiting for transfers between devices: 195 us -> 0 us
  Pallas kernels: 0 us -> 134 us
  blocking collectives: 53.2 us -> 0 us
  matrix products: 31.7 us -> 0 us
  between operations: 18.7 us -> 1.3 us
  local copies, waits for them, and re-layouts: 18.3 us -> 8.52 us
  starting transfers between devices: 4.9 us -> 0 us
    all_to_all x1 -> x0, waiting for transfers between devices: 195 us -> none  [shards(): lax.all_to_all(hidden, 'dp', split_axis=1, concat_axis=0, tiled=True)]
    pallas_call x0 -> x1, Pallas kernels: none -> 134 us  [shards(): pl.pallas_call(functools.partial(kernel, (dp, T, nA, nB, sliced)), out_sh...]
    psum x3 -> x0, blocking collectives: 47.6 us -> none  [the longest x1 23.2 us: shards(): group_wins = lax.psum(local_wins, 'dp')]
    dot_general x3 -> x0, matrix products: 31.7 us -> none  [the longest x1 10.9 us: contract_cols(): lax.dot_general(first_operand, second_operand, (((1,), (1,)), ((), ())),...]
    all_to_all x1 -> x0, local copies, waits for them, and re-layouts: 7.87 us -> none  [shards(): lax.all_to_all(hidden, 'dp', split_axis=1, concat_axis=0, tiled=True)]
    pmax x1 -> x0, blocking collectives: 5.67 us -> none  [shards(): row_top = lax.pmax(jnp.max(logits, axis=1), 'tensor')]
    unnamed x6 -> x4, local copies, waits for them, and re-layouts: 10.2 us -> 5.05 us
    all_to_all x1 -> x0, starting transfers between devices: 4.82 us -> none  [shards(): lax.all_to_all(hidden, 'dp', split_axis=1, concat_axis=0, tiled=True)]
  transfers between devices with their start and end apart: 3 -> 0, of which waited for: 1 -> 0; matrix products, arithmetic and copies ran while one was open for 12% -> 0% of each run, Pallas kernels for 0% -> 0%
where the time goes in v1:
time: 148 us
  Pallas kernels  134 us (91%)
  local copies, waits for them, and re-layouts  8.52 us (6%)
  other arithmetic  4.26 us (3%)
    pallas_call x1, Pallas kernels, shards(): pl.pallas_call(functools.partial(kernel, (dp, T, nA, nB, sliced)), out_sh...  134 us
    unnamed x4, local copies, waits for them, and re-layouts  5.05 us

profile of v1, /device:TPU:0, one launch (start us, length us, event | category | flops | bytes accessed | tf_op | source)
XLA Modules:
  0.0 147.7 jit_solution(2745948731887260441)
XLA Ops:
  1.3 0.7 convert_element_type.29
  1.9 0.7 convert_element_type.32
  2.6 0.7 convert_element_type.28
  3.3 0.8 select_reduce_fusion.1
  4.1 0.1 select_select_fusion
  4.1 0.7 convert_element_type.27
  4.8 0.6 concatenate.3.info
  5.4 0.1 broadcast_in_dim.41
  5.5 0.1 stack_reshape.8
  5.6 0.1 broadcast_in_dim.40
  5.6 0.1 stack_reshape.7
  5.7 0.7 fusion
  6.4 0.1 reshape.51
  6.5 1.3 stack.15.rows
  7.8 133.6 %shard_map.103 = (f32[8,128]{1,0:T(8,128)}, f32[512,1280]{1,0:T(8,128)}, f32[640,1024]{1,0:T(8,128)}) custom-call(bf16[512,5120]{1,0:T(8,128)(2,1)} %hsrc.1, bf16[512,5120]{1,0:T(8,128)(2,1)} %hsrc.1, bf16[5120,1024]{1,0:T(8,128)(2,1)} %w.1, f32[8,512]{1,0:T(8,128)} %stack.15.rows, f32[16,128]{1,0:T(8,128)} %concatenate.3.info), custom_call_target="tpu_custom_call" | custom-call | tf_op jit(solution)/shard_map/pallas_call | solution.py:405
  141.5 1.2 slice.3
  142.6 0.0 copy-start
  142.6 3.6 %copy.14 = f32[512,1280]{1,0:T(8,128)} copy(f32[512,1280]{1,0:T(8,128)} %get-tuple-element.17) | data formatting | bytes 5242880
  146.2 0.0 copy-done
  146.2 1.5 %copy.15 = f32[640,1024]{1,0:T(8,128)} copy(f32[640,1024]{1,0:T(8,128)S(1)} %copy-done) | data formatting | bytes 5242880
  (3 shorter events, 0.0 us)
Async XLA Ops:
  142.6 3.6 %copy-start = (f32[640,1024]{1,0:T(8,128)S(1)}, f32[640,1024]{1,0:T(8,128)}, u32[]{:S(2)}) copy-start(f32[640,1024]{1,0:T(8,128)} %get-tuple-element.18) | copy-start | bytes 7864324

commit v2 on v1

--- a/solution.py
+++ b/solution.py
@@ -15,10 +15,10 @@
 BF16 = jnp.bfloat16
 
 
-def kernel(cfg, hidden, hsrc, w, rows, info, loss_o, gh_o, gw_o,
-           hid_v, w_v, logits, cols, stats, info_all, loss_all, lg_all, hcol, rs_recv,
+def kernel(cfg, hidden, hsrc, w, tok_i, old_i, rew_i, len_i, gid_i, scale_i, loss_o, gh_o, gw_o,
+           hid_v, w_v, logits, cols, rows, stats, info, info_all, loss_all, lg_all, hcol, rs_recv,
            ld, s_info, r_info, s_hid, r_hid, s_x, r_x, s_d, r_d, s_st, r_st,
-           s_loss, r_loss, s_rs, r_rs, s_a, s_b, r_lg):
+           s_loss, r_loss, s_rs, r_rs, s_a, s_b, r_lg, s_t):
     dp, T, nA, nB, sliced = cfg
     R, D = hid_v.shape
     V = w_v.shape[1]
@@ -50,6 +50,37 @@
         load_h(k).start()
         load_w(k).start()
 
+    rolls = rew_i.shape[1]
+    per_roll = R // rolls
+    G8 = info.shape[0]
+    reward_row = rew_i[...].astype(F32)
+    length_row = len_i[...].astype(F32)
+    group_row = gid_i[...].astype(F32)
+    group_of = (lax.broadcasted_iota(jnp.int32, (G8, rolls), 0).astype(F32) == group_row).astype(F32)
+    local_wins = jnp.sum(group_of * reward_row, axis=1, keepdims=True)
+    local_lens = jnp.sum(group_of * length_row, axis=1, keepdims=True)
+    glane = lax.broadcasted_iota(jnp.int32, (G8, 128), 1)
+    info[...] = jnp.where(glane == 0, local_wins, jnp.where(glane == 1, local_lens, 0.0))
+    diag = (
+        lax.broadcasted_iota(jnp.int32, (rolls, rolls), 0) == lax.broadcasted_iota(jnp.int32, (rolls, rolls), 1)
+    ).astype(F32)
+    first = lax.broadcasted_iota(jnp.int32, (rolls, R), 0) * per_roll
+    place = lax.broadcasted_iota(jnp.int32, (rolls, R), 1) - first
+    mine = jnp.logical_and(place >= 0, place < per_roll).astype(F32)
+
+    def spread_row(row):
+        column = jnp.sum(diag * row, axis=1, keepdims=True)
+        return jnp.sum(mine * column, axis=0, keepdims=True)
+
+    place_row = jnp.sum(mine * place.astype(F32), axis=0, keepdims=True)
+    rows[...] = jnp.concatenate(
+        [
+            tok_i[...].astype(F32), old_i[...], spread_row(group_row), spread_row(reward_row),
+            (place_row < spread_row(length_row)).astype(F32), jnp.zeros((3, R), F32),
+        ],
+        axis=0,
+    )
+
     barrier = pltpu.get_barrier_semaphore()
     for d in range(1, dp):
         pl.semaphore_signal(barrier, inc=1, device_id={"dp": (me + d) % dp}, device_id_type=MESH)
@@ -124,7 +155,6 @@
     wins2 = info_all[0]
     for i in range(1, dp):
         wins2 = wins2 + info_all[i]
-    G8 = info.shape[0] - 8
     wins = wins2[0:G8, 0:1]
     lens = wins2[0:G8, 1:2]
     alive = jnp.logical_and(wins > 0.5, wins < GROUP - 0.5).astype(F32)
@@ -132,7 +162,7 @@
     spread = jnp.where(alive > 0.5, jnp.sqrt(wins * (GROUP - wins)) / GROUP, 1.0)
     token_count = jnp.sum(alive * lens, axis=0, keepdims=True)
     divisor = jnp.maximum(token_count, 1.0)
-    factor = info[G8 : G8 + 1, 0:1] / divisor
+    factor = scale_i[...] / divisor
     old = rows[1:2, :]
     gid = rows[2:3, :]
     rew = rows[3:4, :]
@@ -174,31 +204,55 @@
         hit = jnp.where(vcol == cols[r, 0:1], 1.0, 0.0)
         lg_all[me, r, :] = (cols[r, 1:2] * (hit - logits[r, :] * cols[r, 2:3])).astype(BF16)
 
-    def c_up(j):
-        return rcopy(lg_all.at[j], lg_all.at[j], s_a.at[0, j], r_lg.at[j], {"dp": me + nB})
-
-    def c_down(j):
-        return rcopy(lg_all.at[j], lg_all.at[j], s_a.at[1, j], r_lg.at[j], {"dp": me - nB})
-
-    def c_b(j, d):
-        return rcopy(lg_all.at[j], lg_all.at[j], s_b.at[d, j], r_lg.at[j], {"dp": a * nB + (b + d) % nB})
-
-    def recv_lg(j):
-        rcopy(lg_all.at[j], lg_all.at[j], s_a.at[0, j], r_lg.at[j], {"dp": (me + 1) % dp}).wait_recv()
-
-    def send_b(j):
-        for d in range(1, nB):
-            c_b(j, d).start()
-
-    @pl.when(a < nA - 1)
-    def _():
-        c_up(me).start()
-
-    @pl.when(a > 0)
-    def _():
-        c_down(me).start()
-
-    send_b(me)
+    H = R // 2
+    swap = nB == 2 and nA % 2 == 0
+    twin = a + 1 - 2 * (a % 2)
+
+    def half(j, h):
+        return lg_all.at[j, pl.ds(h * H, H), :]
+
+    def c_up(j, h):
+        return rcopy(half(j, h), half(j, h), s_a.at[0, j, h], r_lg.at[j, h], {"dp": me + nB})
+
+    def c_down(j, h):
+        return rcopy(half(j, h), half(j, h), s_a.at[1, j, h], r_lg.at[j, h], {"dp": me - nB})
+
+    def c_b(j, h, d):
+        return rcopy(half(j, h), half(j, h), s_b.at[d, j, h], r_lg.at[j, h], {"dp": a * nB + (b + d) % nB})
+
+    def c_twin():
+        j = a * nB + (b + 1) % nB
+        return rcopy(half(j, 0), half(j, 0), s_t, r_lg.at[j, 0], {"dp": twin * nB + b})
+
+    def recv_lg(j, h):
+        rcopy(half(j, h), half(j, h), s_a.at[0, j, h], r_lg.at[j, h], {"dp": (me + 1) % dp}).wait_recv()
+
+    def each_b(j, h, act):
+        def go():
+            for d in range(1, nB):
+                act(c_b(j, h, d))
+
+        if swap and h == 0:
+            pl.when(j != twin * nB + b)(go)
+        else:
+            go()
+
+    def start(copy):
+        copy.start()
+
+    def done(copy):
+        copy.wait_send()
+
+    for h in range(2):
+        @pl.when(a < nA - 1)
+        def _():
+            c_up(me, h).start()
+
+        @pl.when(a > 0)
+        def _():
+            c_down(me, h).start()
+
+        each_b(me, h, start)
 
     def c_loss(d):
         return rcopy(loss_all.at[me], loss_all.at[me], s_loss.at[d], r_loss.at[me], {"dp": (me + d) % dp})
@@ -214,66 +268,87 @@
             lg_all[me], w_v[pl.ds(col0, GC), :], (((1,), (1,)), ((), ())), preferred_element_type=F32
         )
 
-    @pl.loop(0, (T - 1) * per)
+    other = 2 * x + 1 - c
+
+    def gcols(shard):
+        return hid_v.at[:, pl.ds(pl.multiple_of(shard * CT, CT), CT)]
+
+    def c_pair(xx):
+        return rcopy(gcols(2 * xx + 1 - c), rs_recv.at[xx], s_rs.at[xx], r_rs.at[xx], {"tensor": other})
+
+    def wait_pair(xx):
+        rcopy(gcols(2 * xx + c), rs_recv.at[xx], s_rs.at[xx], r_rs.at[xx], {"tensor": other}).wait_recv()
+
+    def c_rs(d):
+        peer = ((x + d) % nX) * 2 + c
+        return rcopy(gcols(peer), rs_recv.at[nX + x], s_rs.at[nX + d], r_rs.at[nX + x], {"tensor": peer})
+
+    @pl.loop(0, nX * per)
     def _(n):
-        peer = (t + 1 + n // per) % T
-        col0 = pl.multiple_of(peer * CT + (n % per) * GC, GC)
+        col0 = pl.multiple_of((2 * (n // per) + 1 - c) * CT + (n % per) * GC, GC)
         hid_v[:, pl.ds(col0, GC)] = gh_dot(col0).astype(BF16)
 
-    own_hid.wait()
-    for d in range(1, dp):
-        i = (me + d) % dp
-        rcopy(hslice(i), hcol.at[i, qrows(t), :], s_hid.at[d], r_hid.at[i], {"dp": i}).wait_recv()
-
-    def c_x(d):
-        q = hcol.at[:, qrows(t), :]
-        return rcopy(q, q, s_x.at[d], r_x.at[x], {"tensor": ((x + d) % nX) * 2 + c})
-
-    def c_d(xx):
-        q = hcol.at[:, qrows(2 * xx + c), :]
-        return rcopy(q, q, s_d.at[xx], r_d.at[xx], {"tensor": 2 * x + 1 - c})
-
-    for d in range(1, nX):
-        c_x(d).start()
-    c_d(x).start()
-
-    def c_rs(d):
-        peer = (t + d) % T
-        return rcopy(
-            hid_v.at[:, pl.ds(pl.multiple_of(peer * CT, CT), CT)],
-            rs_recv.at[t], s_rs.at[d], r_rs.at[t], {"tensor": peer},
-        )
-
-    for d in range(1, T):
-        c_rs(d).start()
+    for xx in range(nX):
+        c_pair(xx).start()
 
     @pl.loop(0, per)
     def _(n):
         off = pl.multiple_of(n * GC, GC)
         gh_o[:, pl.ds(off, GC)] = gh_dot(pl.multiple_of(t * CT + off, GC))
 
+    for xx in range(nX):
+        wait_pair(xx)
+
+    @pl.loop(0, (nX - 1) * per)
+    def _(n):
+        xx = (x + 1 + n // per) % nX
+        off = pl.multiple_of((n % per) * GC, GC)
+        col0 = pl.multiple_of((2 * xx + c) * CT + off, GC)
+        hid_v[:, pl.ds(col0, GC)] = (gh_dot(col0) + rs_recv[xx, :, pl.ds(off, GC)].astype(F32)).astype(BF16)
+
+    own_hid.wait()
+    for d in range(1, dp):
+        i = (me + d) % dp
+        rcopy(hslice(i), hcol.at[i, qrows(t), :], s_hid.at[d], r_hid.at[i], {"dp": i}).wait_recv()
+
+    def c_x(d):
+        q = hcol.at[:, qrows(t), :]
+        return rcopy(q, q, s_x.at[d], r_x.at[x], {"tensor": ((x + d) % nX) * 2 + c})
+
+    def c_d(xx):
+        q = hcol.at[:, qrows(2 * xx + c), :]
+        return rcopy(q, q, s_d.at[xx], r_d.at[xx], {"tensor": 2 * x + 1 - c})
+
+    for d in range(1, nX):
+        c_x(d).start()
+    c_d(x).start()
+
+    for d in range(1, nX):
+        c_rs(d).start()
+
     def relay(s):
-        @pl.when(a >= s)
-        def _():
-            j = me - s * nB
-            recv_lg(j)
-
-            @pl.when(a < nA - 1)
+        for h in range(2):
+            @pl.when(a >= s)
             def _():
-                c_up(j).start()
-
-            send_b(j)
-
-        @pl.when(a + s < nA)
-        def _():
-            j = me + s * nB
-            recv_lg(j)
-
-            @pl.when(a > 0)
+                j = me - s * nB
+                recv_lg(j, h)
+
+                @pl.when(a < nA - 1)
+                def _():
+                    c_up(j, h).start()
+
+                each_b(j, h, start)
+
+            @pl.when(a + s < nA)
             def _():
-                c_down(j).start()
-
-            send_b(j)
+                j = me + s * nB
+                recv_lg(j, h)
+
+                @pl.when(a > 0)
+                def _():
+                    c_down(j, h).start()
+
+                each_b(j, h, start)
 
     def gw_add(j):
         gw_o[...] += lax.dot_general(
@@ -292,11 +367,16 @@
                 @pl.when(jnp.logical_and(aa >= 0, aa < nA))
                 def _():
                     if d > 0:
-                        recv_lg(j)
+                        if not (swap and s == 0):
+                            recv_lg(j, 0)
+                        recv_lg(j, 1)
                     gw_add(j)
 
     relay(1)
     relay(2)
+    if swap:
+        recv_lg(a * nB + (b + 1) % nB, 0)
+        c_twin().start()
     for d in range(1, nX):
         xx = (x + d) % nX
         q = hcol.at[:, qrows(2 * xx + c), :]
@@ -312,16 +392,16 @@
     for s in range(1, nA - 1):
         add_steps([(s, d) for d in range(1, nB)])
 
-    for d in range(1, T):
-        i = (t + d) % T
-        rcopy(hid_v.at[:, pl.ds(0, CT)], rs_recv.at[i], s_rs.at[d], r_rs.at[i], {"tensor": i}).wait_recv()
+    for d in range(1, nX):
+        xx = (x + d) % nX
+        rcopy(gcols(t), rs_recv.at[nX + xx], s_rs.at[nX + d], r_rs.at[nX + xx], {"tensor": 2 * xx + c}).wait_recv()
 
     @pl.loop(0, R // RC)
     def _(n):
         r = pl.ds(pl.multiple_of(n * RC, RC), RC)
-        acc = gh_o[r, :]
-        for d in range(1, T):
-            acc = acc + rs_recv[(t + d) % T, r, :].astype(F32)
+        acc = gh_o[r, :] + rs_recv[x, r, :].astype(F32)
+        for d in range(1, nX):
+            acc = acc + rs_recv[nX + (x + d) % nX, r, :].astype(F32)
         gh_o[r, :] = acc
 
     for d in range(1, dp):
@@ -330,7 +410,7 @@
     loss = loss_all[0]
     for i in range(1, dp):
         loss = loss + loss_all[i]
-    loss_o[...] = loss / divisor
+    loss_o[...] = loss[0:1, 0:1] / divisor
 
     add_steps([(nA - 1, d) for d in range(1, nB)])
 
@@ -340,34 +420,41 @@
         c_loss(d).wait_send()
     for d in range(1, T):
         c_st(d).wait_send()
-        c_rs(d).wait_send()
     for d in range(1, nX):
         c_x(d).wait_send()
+        c_rs(d).wait_send()
     for xx in range(nX):
         c_d(xx).wait_send()
+        c_pair(xx).wait_send()
+    if swap:
+        c_twin().wait_send()
     for s in range(nA):
-        @pl.when(a >= s)
+        for h in range(2):
+            @pl.when(a >= s)
+            def _():
+                j = me - s * nB
+
+                @pl.when(a < nA - 1)
+                def _():
+                    c_up(j, h).wait_send()
+
+                each_b(j, h, done)
+
+            if s > 0:
+                @pl.when(a + s < nA)
+                def _():
+                    j = me + s * nB
+
+                    @pl.when(a > 0)
+                    def _():
+                        c_down(j, h).wait_send()
+
+                    each_b(j, h, done)
+
+    for h in range(2):
+        @pl.when(a > 0)
         def _():
-            j = me - s * nB
-
-            @pl.when(a < nA - 1)
-            def _():
-                c_up(j).wait_send()
-
-            for d in range(1, nB):
-                c_b(j, d).wait_send()
-
-        @pl.when(a + s < nA)
-        def _():
-            j = me + s * nB
-
-            @pl.when(a > 0)
-            def _():
-                c_down(j).wait_send()
-
-            if s > 0:
-                for d in range(1, nB):
-                    c_b(j, d).wait_send()
+            c_down(me, h).wait_send()
 
 
 def shards(hidden, head_weight, token_ids, old_logprob, rewards, lengths, group_ids, loss_scale):
@@ -382,19 +469,6 @@
     G8 = -(-groups // 8) * 8
     C = D // dp
     sliced = C % 128 == 0
-    response = R // rolls
-    member = (group_ids[None, :] == jnp.arange(G8, dtype=jnp.int32)[:, None]).astype(F32)
-    wins = jnp.sum(member * rewards.astype(F32)[None, :], axis=1)
-    lens = jnp.sum(member * lengths.astype(F32)[None, :], axis=1)
-    lane = jnp.arange(128)[None, :]
-    info = jnp.where(lane == 0, wins[:, None], jnp.where(lane == 1, lens[:, None], 0.0))
-    info = jnp.concatenate([info, jnp.full((8, 128), 1.0, F32) * loss_scale], axis=0)
-    inside = (jnp.arange(response, dtype=jnp.int32)[None, :] < lengths[:, None]).astype(F32).reshape(R)
-    spread = lambda v: jnp.broadcast_to(v.astype(F32)[:, None], (rolls, response)).reshape(R)
-    zero = jnp.zeros((R,), F32)
-    rows = jnp.stack(
-        [token_ids.astype(F32), old_logprob, spread(group_ids), spread(rewards), inside, zero, zero, zero]
-    )
     if sliced:
         hsrc = hidden
     else:
@@ -405,19 +479,21 @@
     loss, gh, gw = pl.pallas_call(
         functools.partial(kernel, (dp, T, nA, nB, sliced)),
         out_shape=(
-            jax.ShapeDtypeStruct((8, 128), F32),
+            jax.ShapeDtypeStruct((1, 1), F32),
             jax.ShapeDtypeStruct((R, D // T), F32),
             jax.ShapeDtypeStruct((C, V), F32),
         ),
-        in_specs=[anyw, anyw, anyw, vm, vm],
+        in_specs=[anyw] * 3 + [vm] * 6,
         out_specs=(vm, vm, vm),
         scratch_shapes=[
             pltpu.VMEM((R, D), BF16),
             pltpu.VMEM((D, V), BF16),
             pltpu.VMEM((R, V), F32),
             pltpu.VMEM((R, 128), F32),
+            pltpu.VMEM((8, R), F32),
             pltpu.VMEM((T, 8, R), F32),
-            pltpu.VMEM((dp, G8 + 8, 128), F32),
+            pltpu.VMEM((G8, 128), F32),
+            pltpu.VMEM((dp, G8, 128), F32),
             pltpu.VMEM((dp, 8, 128), F32),
             pltpu.VMEM((dp, R, V), BF16),
             pltpu.VMEM((dp, R, C), BF16),
@@ -430,13 +506,17 @@
             dma((T,)), dma((T,)),
             dma((dp,)), dma((dp,)),
             dma((T,)), dma((T,)),
-            dma((2, dp)), dma((nB, dp)), dma((dp,)),
+            dma((2, dp, 2)), dma((nB, dp, 2)), dma((dp, 2)), dma(()),
         ],
         compiler_params=pltpu.CompilerParams(
             collective_id=0, has_side_effects=True, vmem_limit_bytes=63 * 1024 * 1024
         ),
-    )(hidden, hsrc, head_weight, rows, info)
-    return (loss[0, 0], gh, gw)
+    )(
+        hidden, hsrc, head_weight, token_ids.reshape(1, R), old_logprob.reshape(1, R),
+        rewards.reshape(1, rolls), lengths.reshape(1, rolls), group_ids.reshape(1, rolls),
+        loss_scale.reshape(1, 1),
+    )
+    return (loss.reshape(()), gh, gw)
 
 
 def solution(mesh):

time: 148 us -> 128 us (0.86)
  the two profiles are of different devices: /device:TPU:0 before, /device:TPU:25 now
where the time goes in v2:
time: 128 us
  Pallas kernels  120 us (94%)
  local copies, waits for them, and re-layouts  5.05 us (4%)
  between operations  3.12 us (2%)
    pallas_call x1, Pallas kernels, shards(): pl.pallas_call(functools.partial(kernel, (dp, T, nA, nB, sliced)), out_sh...  120 us
    unnamed x4, local copies, waits for them, and re-layouts  5.05 us

profile of v2, /device:TPU:25, one launch (start us, length us, event | category | flops | bytes accessed | tf_op | source)
XLA Modules:
  0.0 128.3 jit_solution(8817142167261618890)
XLA Ops:
  1.3 120.1 %shard_map.103 = (f32[1,1]{1,0:T(1,128)}, f32[512,1280]{1,0:T(8,128)}, f32[640,1024]{1,0:T(8,128)}) custom-call(bf16[512,5120]{1,0:T(8,128)(2,1)} %hsrc.1, bf16[512,5120]{1,0:T(8,128)(2,1)} %hsrc.1, bf16[5120,1024]{1,0:T(8,128)(2,1)} %w.1, s32[1,512]{1,0:T(1,128)} %bitcast.8, f32[1,512]{1,0:T(1,128)} %bitcast.9, s32[1,8]{1,0:T(1,128)} %bitcast.10, ...), custom_call_target="tpu_custom_call" | custom-call | tf_op jit(solution)/shard_map/pallas_call | solution.py:479
  122.1 0.0 copy-start
  122.1 3.6 %copy.16 = f32[512,1280]{1,0:T(8,128)} copy(f32[512,1280]{1,0:T(8,128)} %get-tuple-element.13) | data formatting | bytes 5242880
  125.7 0.0 copy-done
  125.7 1.5 %copy.17 = f32[640,1024]{1,0:T(8,128)} copy(f32[640,1024]{1,0:T(8,128)S(1)} %copy-done) | data formatting | bytes 5242880
Async XLA Ops:
  122.1 3.6 %copy-start = (f32[640,1024]{1,0:T(8,128)S(1)}, f32[640,1024]{1,0:T(8,128)}, u32[]{:S(2)}) copy-start(f32[640,1024]{1,0:T(8,128)} %get-tuple-element.14) | copy-start | bytes 7864324

commit v3 on v2

--- a/solution.py
+++ b/solution.py
@@ -115,95 +115,6 @@
     pad = jnp.zeros((128 - rows.shape[0], R), F32)
     cols[...] = jnp.transpose(jnp.concatenate([rows[...], pad], axis=0))
 
-    logits[...] = jnp.zeros_like(logits)
-
-    @pl.loop(0, NK)
-    def _(k):
-        s = pl.ds(pl.multiple_of(k * KC, KC), KC)
-        load_h(k).wait()
-        load_w(k).wait()
-        logits[...] += jnp.dot(hid_v[:, s], w_v[s, :], preferred_element_type=F32)
-
-    RC = 32
-    lane = lax.broadcasted_iota(jnp.int32, (RC, 128), 1)
-    vcol = lax.broadcasted_iota(jnp.int32, (RC, V), 1).astype(F32) + (t * V).astype(F32)
-
-    @pl.loop(0, R // RC)
-    def _(n):
-        r = pl.ds(pl.multiple_of(n * RC, RC), RC)
-        lo = logits[r, :]
-        tok = cols[r, 0:1]
-        top = jnp.max(lo, axis=1, keepdims=True)
-        target = jnp.sum(jnp.where(vcol == tok, lo, 0.0), axis=1, keepdims=True)
-        e = jnp.exp(lo - top)
-        total = jnp.sum(e, axis=1, keepdims=True)
-        logits[r, :] = e
-        cols[r, :] = jnp.where(
-            lane == 0, tok, jnp.where(lane == 1, top, jnp.where(lane == 2, total, jnp.where(lane == 3, target, 0.0)))
-        )
-
-    stats[t] = jnp.transpose(cols[...])[0:8, :]
-
-    def c_st(d):
-        return rcopy(stats.at[t], stats.at[t], s_st.at[d], r_st.at[t], {"tensor": (t + d) % T})
-
-    for d in range(1, T):
-        c_st(d).start()
-    for d in range(1, dp):
-        i = (me + d) % dp
-        rcopy(info, info_all.at[i], s_info.at[d], r_info.at[i], {"dp": i}).wait_recv()
-    wins2 = info_all[0]
-    for i in range(1, dp):
-        wins2 = wins2 + info_all[i]
-    wins = wins2[0:G8, 0:1]
-    lens = wins2[0:G8, 1:2]
-    alive = jnp.logical_and(wins > 0.5, wins < GROUP - 0.5).astype(F32)
-    center = wins / GROUP
-    spread = jnp.where(alive > 0.5, jnp.sqrt(wins * (GROUP - wins)) / GROUP, 1.0)
-    token_count = jnp.sum(alive * lens, axis=0, keepdims=True)
-    divisor = jnp.maximum(token_count, 1.0)
-    factor = scale_i[...] / divisor
-    old = rows[1:2, :]
-    gid = rows[2:3, :]
-    rew = rows[3:4, :]
-    inside = rows[4:5, :]
-    member = (lax.broadcasted_iota(jnp.int32, (G8, R), 0).astype(F32) == gid).astype(F32)
-    roll_alive = jnp.sum(member * alive, axis=0, keepdims=True)
-    roll_center = jnp.sum(member * center, axis=0, keepdims=True)
-    roll_spread = jnp.sum(member * spread, axis=0, keepdims=True)
-    adv = roll_alive * (rew - roll_center) / roll_spread
-    weight = roll_alive * inside
-
-    for d in range(1, T):
-        i = (t + d) % T
-        rcopy(stats.at[i], stats.at[i], s_st.at[d], r_st.at[i], {"tensor": i}).wait_recv()
-    top = stats[0, 1:2, :]
-    for i in range(1, T):
-        top = jnp.maximum(top, stats[i, 1:2, :])
-    total = jnp.zeros_like(top)
-    target = jnp.zeros_like(top)
-    for i in range(T):
-        total = total + stats[i, 2:3, :] * jnp.exp(stats[i, 1:2, :] - top)
-        target = target + stats[i, 3:4, :]
-    log_prob = target - top - jnp.log(total)
-    ratio = jnp.exp(log_prob - old)
-    clipped = jnp.clip(ratio, 1.0 - clip_low, 1.0 + clip_high)
-    token_loss = -jnp.minimum(ratio * adv, clipped * adv)
-    active = ratio * adv <= clipped * adv
-    coef = jnp.where(active, -adv * ratio, 0.0) * weight * factor
-    mytop = stats[t][1:2, :]
-    scale = jnp.exp(mytop - top) / total
-    loss_all[me] = jnp.broadcast_to(jnp.sum(weight * token_loss, axis=1, keepdims=True), (8, 128))
-    cols[...] = jnp.transpose(
-        jnp.concatenate([rows[0:1, :], coef, scale, jnp.zeros((125, R), F32)], axis=0)
-    )
-
-    @pl.loop(0, R // RC)
-    def _(n):
-        r = pl.ds(pl.multiple_of(n * RC, RC), RC)
-        hit = jnp.where(vcol == cols[r, 0:1], 1.0, 0.0)
-        lg_all[me, r, :] = (cols[r, 1:2] * (hit - logits[r, :] * cols[r, 2:3])).astype(BF16)
-
     H = R // 2
     swap = nB == 2 and nA % 2 == 0
     twin = a + 1 - 2 * (a % 2)
@@ -243,7 +154,101 @@
     def done(copy):
         copy.wait_send()
 
+    logits[...] = jnp.zeros_like(logits)
+    RC = 32
+    lane = lax.broadcasted_iota(jnp.int32, (RC, 128), 1)
+    vcol = lax.broadcasted_iota(jnp.int32, (RC, V), 1).astype(F32) + (t * V).astype(F32)
+    loss_sum = jnp.zeros((1, 1), F32)
+
+    def c_st(h, d):
+        return rcopy(stats.at[h, t], stats.at[h, t], s_st.at[h, d], r_st.at[h, t], {"tensor": (t + d) % T})
+
     for h in range(2):
+        rh = pl.ds(h * H, H)
+        hs = slice(h * H, (h + 1) * H)
+
+        @pl.loop(0, NK)
+        def _(k):
+            s = pl.ds(pl.multiple_of(k * KC, KC), KC)
+            if h == 0:
+                load_h(k).wait()
+                load_w(k).wait()
+            logits[rh, :] += jnp.dot(hid_v[rh, s], w_v[s, :], preferred_element_type=F32)
+
+        @pl.loop(0, H // RC)
+        def _(n):
+            r = pl.ds(pl.multiple_of(h * H + n * RC, RC), RC)
+            lo = logits[r, :]
+            tok = cols[r, 0:1]
+            top = jnp.max(lo, axis=1, keepdims=True)
+            target = jnp.sum(jnp.where(vcol == tok, lo, 0.0), axis=1, keepdims=True)
+            e = jnp.exp(lo - top)
+            total = jnp.sum(e, axis=1, keepdims=True)
+            logits[r, :] = e
+            cols[r, :] = jnp.where(
+                lane == 0, tok, jnp.where(lane == 1, top, jnp.where(lane == 2, total, jnp.where(lane == 3, target, 0.0)))
+            )
+
+        stats[h, t] = jnp.transpose(cols[rh, :])[0:8, :]
+        for d in range(1, T):
+            c_st(h, d).start()
+        if h == 0:
+            for d in range(1, dp):
+                i = (me + d) % dp
+                rcopy(info, info_all.at[i], s_info.at[d], r_info.at[i], {"dp": i}).wait_recv()
+            wins2 = info_all[0]
+            for i in range(1, dp):
+                wins2 = wins2 + info_all[i]
+            wins = wins2[0:G8, 0:1]
+            lens = wins2[0:G8, 1:2]
+            alive = jnp.logical_and(wins > 0.5, wins < GROUP - 0.5).astype(F32)
+            center = wins / GROUP
+            spread = jnp.where(alive > 0.5, jnp.sqrt(wins * (GROUP - wins)) / GROUP, 1.0)
+            token_count = jnp.sum(alive * lens, axis=0, keepdims=True)
+            divisor = jnp.maximum(token_count, 1.0)
+            factor = scale_i[...] / divisor
+            old = rows[1:2, :]
+            gid = rows[2:3, :]
+            rew = rows[3:4, :]
+            inside = rows[4:5, :]
+            member = (lax.broadcasted_iota(jnp.int32, (G8, R), 0).astype(F32) == gid).astype(F32)
+            roll_alive = jnp.sum(member * alive, axis=0, keepdims=True)
+            roll_center = jnp.sum(member * center, axis=0, keepdims=True)
+            roll_spread = jnp.sum(member * spread, axis=0, keepdims=True)
+            adv = roll_alive * (rew - roll_center) / roll_spread
+            weight = roll_alive * inside
+
+        for d in range(1, T):
+            i = (t + d) % T
+            rcopy(stats.at[h, i], stats.at[h, i], s_st.at[h, d], r_st.at[h, i], {"tensor": i}).wait_recv()
+        top = stats[h, 0, 1:2, :]
+        for i in range(1, T):
+            top = jnp.maximum(top, stats[h, i, 1:2, :])
+        total = jnp.zeros_like(top)
+        target = jnp.zeros_like(top)
+        for i in range(T):
+            total = total + stats[h, i, 2:3, :] * jnp.exp(stats[h, i, 1:2, :] - top)
+            target = target + stats[h, i, 3:4, :]
+        adv_h, weight_h = adv[:, hs], weight[:, hs]
+        log_prob = target - top - jnp.log(total)
+        ratio = jnp.exp(log_prob - old[:, hs])
+        clipped = jnp.clip(ratio, 1.0 - clip_low, 1.0 + clip_high)
+        token_loss = -jnp.minimum(ratio * adv_h, clipped * adv_h)
+        active = ratio * adv_h <= clipped * adv_h
+        coef = jnp.where(active, -adv_h * ratio, 0.0) * weight_h * factor
+        mytop = stats[h, t][1:2, :]
+        scale = jnp.exp(mytop - top) / total
+        loss_sum = loss_sum + jnp.sum(weight_h * token_loss, axis=1, keepdims=True)
+        cols[rh, :] = jnp.transpose(
+            jnp.concatenate([rows[0:1, hs], coef, scale, jnp.zeros((125, H), F32)], axis=0)
+        )
+
+        @pl.loop(0, H // RC)
+        def _(n):
+            r = pl.ds(pl.multiple_of(h * H + n * RC, RC), RC)
+            hit = jnp.where(vcol == cols[r, 0:1], 1.0, 0.0)
+            lg_all[me, r, :] = (cols[r, 1:2] * (hit - logits[r, :] * cols[r, 2:3])).astype(BF16)
+
         @pl.when(a < nA - 1)
         def _():
             c_up(me, h).start()
@@ -253,6 +258,8 @@
             c_down(me, h).start()
 
         each_b(me, h, start)
+
+    loss_all[me] = jnp.broadcast_to(loss_sum, (8, 128))
 
     def c_loss(d):
         return rcopy(loss_all.at[me], loss_all.at[me], s_loss.at[d], r_loss.at[me], {"dp": (me + d) % dp})
@@ -419,7 +426,8 @@
         c_hid(d).wait_send()
         c_loss(d).wait_send()
     for d in range(1, T):
-        c_st(d).wait_send()
+        for h in range(2):
+            c_st(h, d).wait_send()
     for d in range(1, nX):
         c_x(d).wait_send()
         c_rs(d).wait_send()
@@ -491,7 +499,7 @@
             pltpu.VMEM((R, V), F32),
             pltpu.VMEM((R, 128), F32),
             pltpu.VMEM((8, R), F32),
-            pltpu.VMEM((T, 8, R), F32),
+            pltpu.VMEM((2, T, 8, R // 2), F32),
             pltpu.VMEM((G8, 128), F32),
             pltpu.VMEM((dp, G8, 128), F32),
             pltpu.VMEM((dp, 8, 128), F32),
@@ -503,7 +511,7 @@
             dma((dp,)), dma((dp,)),
             dma((T,)), dma((T,)),
             dma((T,)), dma((T,)),
-            dma((T,)), dma((T,)),
+            dma((2, T)), dma((2, T)),
             dma((dp,)), dma((dp,)),
             dma((T,)), dma((T,)),
             dma((2, dp, 2)), dma((nB, dp, 2)), dma((dp, 2)), dma(()),

time: 128 us -> 124 us (0.969)
  the two profiles are of different devices: /device:TPU:25 before, /device:TPU:0 now
where the time goes in v3:
time: 124 us
  Pallas kernels  116 us (94%)
  local copies, waits for them, and re-layouts  5.05 us (4%)
  between operations  3.12 us (3%)
    pallas_call x1, Pallas kernels, shards(): pl.pallas_call(functools.partial(kernel, (dp, T, nA, nB, sliced)), out_sh...  116 us
    unnamed x4, local copies, waits for them, and re-layouts  5.05 us

profile of v3, /device:TPU:0, one launch (start us, length us, event | category | flops | bytes accessed | tf_op | source)
XLA Modules:
  0.0 124.1 jit_solution(16952347406712823932)
XLA Ops:
  1.3 116.0 %shard_map.103 = (f32[1,1]{1,0:T(1,128)}, f32[512,1280]{1,0:T(8,128)}, f32[640,1024]{1,0:T(8,128)}) custom-call(bf16[512,5120]{1,0:T(8,128)(2,1)} %hsrc.1, bf16[512,5120]{1,0:T(8,128)(2,1)} %hsrc.1, bf16[5120,1024]{1,0:T(8,128)(2,1)} %w.1, s32[1,512]{1,0:T(1,128)} %bitcast.8, f32[1,512]{1,0:T(1,128)} %bitcast.9, s32[1,8]{1,0:T(1,128)} %bitcast.10, ...), custom_call_target="tpu_custom_call" | custom-call | tf_op jit(solution)/shard_map/pallas_call | solution.py:487
  118.0 0.0 copy-start
  118.0 3.6 %copy.16 = f32[512,1280]{1,0:T(8,128)} copy(f32[512,1280]{1,0:T(8,128)} %get-tuple-element.13) | data formatting | bytes 5242880
  121.5 0.0 copy-done
  121.5 1.5 %copy.17 = f32[640,1024]{1,0:T(8,128)} copy(f32[640,1024]{1,0:T(8,128)S(1)} %copy-done) | data formatting | bytes 5242880
Async XLA Ops:
  118.0 3.6 %copy-start = (f32[640,1024]{1,0:T(8,128)S(1)}, f32[640,1024]{1,0:T(8,128)}, u32[]{:S(2)}) copy-start(f32[640,1024]{1,0:T(8,128)} %get-tuple-element.14) | copy-start | bytes 7864324
